TPU v7x, 256 devices: a whole 4x4x8 slice. The times are simulated.
256 devices in a mesh: ga: 64 (over y_hi, z, x), ta: 4 (over y_lo, core).
Axes of the slice: x: 4, y: 4 (y_hi: 2, y_lo: 2; y = y_hi * 2 + y_lo), z: 8, core: 2. Of those that a mesh axis runs over, the one named last changes fastest.
Arguments:
- density: bfloat16 [2, 6144, 16384], P(None, 'ga', 'ta'), may hold values from -6 to 6
- coulomb: float32 [6144], P('ga'), may hold values from 0.001275776 to 0.01275776
- row_block: int32 [1], replicated, may hold values from 0 to 67
Outputs:
- kernel: float32 [4, 4096, 2, 240], P('ta', 'ga')
Inputs may be any that keep to these rules, and one draw needn't show every extreme that they name: The rows row_block * 240 to row_block * 240 + 239 lie among the 16384 transitions.
All inputs are finite; a program needn't handle non-finite values.
Results may differ from a plain program's by a relative error of at most 0.0025.
Values may be sent and summed in bfloat16 or wider, within the bound.
A program may use at most 64 MiB of HBM per device.

v0:
```python
import jax
import jax.numpy as jnp
from jax import lax
from jax.sharding import Mesh
from jax.sharding import PartitionSpec as P

RB = 240
GA = ("ga_0", "ga_1", "ga_2")


def from_everyone(x, axis):
    peers = lax.axis_size(axis)
    return lax.all_to_all(jnp.broadcast_to(x[None], (peers, *x.shape)), axis, 0, 0, tiled=True)


def taken_together(x, axis):
    everything = from_everyone(x, axis)
    return jnp.sum(everything.astype(jnp.float32), axis=0)


def joined_along(pieces, dim):
    pieces = jnp.moveaxis(pieces, 0, dim)
    shape = pieces.shape
    return pieces.reshape(*shape[:dim], shape[dim] * shape[dim + 1], *shape[dim + 2 :])


def all_blocks(x, axes, turns):
    pieces = x[None]
    for k in turns:
        pieces = lax.all_gather(pieces, axes[k], axis=0, tiled=True)
    block = [lax.axis_size(axes[k]) for k in reversed(turns)]
    pieces = pieces.reshape(*block, *x.shape)
    turned = sorted(range(len(turns)), key=lambda place: turns[len(turns) - 1 - place])
    return pieces.transpose(*turned, *range(len(turns), pieces.ndim)).reshape(-1, *x.shape)


def gather_axes(x, axes, turns, dim):
    return joined_along(all_blocks(x, axes, turns), dim)


def stack_left(folded):
    real_part = folded[0]
    imag_part = folded[1]
    upper_half = jnp.concatenate([real_part, -imag_part], axis=1)
    lower_half = jnp.concatenate([imag_part, real_part], axis=1)
    return jnp.concatenate([upper_half, lower_half], axis=0)


def body(density, coulomb, row_block):
    col_width = density.shape[2]
    group_index = lax.axis_index("ta")
    column = row_block[0] * RB + jnp.arange(RB, dtype=jnp.int32)
    owner_index = column // col_width
    position = jnp.clip(column - group_index * col_width, 0, col_width - 1)
    picked = jnp.take(density, position, axis=2)
    weighted = (coulomb[None, :, None] * picked.astype(jnp.float32)).astype(jnp.bfloat16)
    masked = jnp.where(
        (owner_index == group_index)[None, None, :], weighted.astype(jnp.float32), 0.0
    )
    folded = (
        taken_together(masked.astype(jnp.bfloat16), "ta").astype(jnp.float32).astype(jnp.bfloat16)
    )
    columns = lax.all_to_all(density, GA, split_axis=2, concat_axis=1, tiled=True)
    own_cols = columns.shape[2]
    whole_rows = gather_axes(folded, GA, (0, 1, 2), 1)
    all_g = whole_rows.shape[1]
    flattened = columns.reshape(2 * all_g, own_cols)
    kernel = lax.dot_general(
        flattened,
        stack_left(whole_rows),
        (((0,), (0,)), ((), ())),
        preferred_element_type=jnp.float32,
    )
    return kernel.reshape(1, kernel.shape[0], 2, RB)


def solution(mesh):
    split = Mesh(mesh.devices.reshape(2, 8, 4, mesh.shape["ta"]), ("ga_0", "ga_1", "ga_2", "ta"))
    in_specs = (P(None, GA, "ta"), P(GA), P())
    out_specs = P("ta", GA, None, None)
    return jax.shard_map(body, mesh=split, in_specs=in_specs, out_specs=out_specs, check_vma=False)
```

profile of v0, /device:TPU:16, one launch (start us, length us, event | category | flops | bytes accessed | tf_op | source)
XLA Modules:
  0.0 175.1 jit_solution(18166927646175314652)
XLA Ops:
  6.5 0.0 copy-start.1
  6.5 0.0 all-gather.4.cloned.1.call-start
  7.3 5.2 %copy.19 = bf16[2,96,4096]{1,0,2:T(2,128)(2,1)S(1)} copy(bf16[2,96,4096]{2,1,0:T(8,128)(2,1)} %param.3) | data formatting | bytes 3145728 | tf_op args[0]
  12.5 0.9 gather_fusion
  13.4 0.0 copy-done.1
  13.4 1.2 fusion.11
  14.6 0.1 copy.20
  14.7 9.8 %all_to_all.20 = bf16[4,2,96,240]{3,2,1,0:T(8,128)(2,1)S(1)} all-to-all(bf16[4,2,96,240]{3,2,1,0:T(8,128)(2,1)S(1)} %broadcast_in_dim.37), channel_id=1, replica_groups=mesh['ga_0'=2,'ga_1'=8,'ga_2'=4,'ta'=4] {'ta'}, dimensions={0} | all-to-all | bytes 737280 | tf_op jit(solution)/shard_map/all_to_all | solution.py:13
  24.5 0.1 reduce_sum.12
  24.6 6.9 %all-gather = bf16[4,96,240]{2,1,0:T(8,128)(2,1)} all-gather(bf16[2,96,240]{2,1,0:T(8,128)(2,1)S(1)} %reduce_sum.12), channel_id=2, replica_groups=mesh['ga_0'=2,'ga_1'=8,'ga_2'=4,'ta'=4] {'ga_0'}, dimensions={0}, use_global_device_ids=true | all-gather | bytes 276480 | tf_op jit(solution)/shard_map/all_gather | solution.py:30
  31.5 0.0 all-gather.4.cloned.1.call-update
  31.5 0.0 all-gather.6.cloned.1.call-start
  31.6 42.4 %all-gather.4.cloned.1.call-done = bf16[16,2,96,240]{3,2,1,0:T(8,128)(2,1)} async-done(((bf16[2,2,96,240]{3,2,1,0:T(8,128)(2,1)}), bf16[16,2,96,240]{3,2,1,0:T(8,128)(2,1)}) %all-gather.4.cloned.1.call-update) | async-done | bytes 1474576 | tf_op jit(solution)/shard_map/all_gather | solution.py:30
  74.0 0.0 all-gather.6.cloned.1.call-update
  74.0 55.2 %all_to_all.21 = bf16[2,96,4096]{1,0,2:T(2,128)(2,1)S(1)} all-to-all(bf16[2,96,4096]{1,0,2:T(2,128)(2,1)S(1)} %copy.19), channel_id=1, replica_groups=mesh['ga_0'=2,'ga_1'=8,'ga_2'=4,'ta'=4] {'ga_0','ga_1','ga_2'}, dimensions={2} | all-to-all | bytes 3145728 | tf_op jit(solution)/shard_map/all_to_all | solution.py:63
  129.3 0.3 copy.23
  129.6 1.4 copy.24
  130.9 3.8 %reshape.79 = bf16[12288,64]{0,1:T(8,128)(2,1)} reshape(bf16[2,64,96,64]{2,1,0,3:T(8,128)(2,1)S(1)} %copy.24) | data formatting | bytes 3145728 | tf_op jit(solution)/shard_map/reshape | solution.py:67
  134.8 23.8 %all-gather.6.cloned.1.call-done = bf16[64,2,96,240]{3,2,1,0:T(8,128)(2,1)} async-done(((bf16[16,2,96,240]{3,2,1,0:T(8,128)(2,1)}), bf16[64,2,96,240]{3,2,1,0:T(8,128)(2,1)}) %all-gather.6.cloned.1.call-update) | async-done | bytes 5898256 | tf_op jit(solution)/shard_map/all_gather | solution.py:30
  158.5 3.2 %copy.21 = bf16[2,8,4,2,96,240]{5,4,3,2,1,0:T(8,128)(2,1)S(1)} copy(bf16[2,8,4,2,96,240]{5,4,3,0,1,2:T(8,128)(2,1)} %bitcast.27) | data formatting | bytes 11796480 | tf_op jit(solution)/shard_map/transpose | solution.py:34
  161.8 0.5 fusion.14
  162.3 0.0 copy-start
  162.3 0.4 bitcast_negate_fusion
  162.7 1.0 copy-done
  163.7 3.7 %fusion.8 = f32[64,480]{1,0:T(8,128)S(1)} fusion(bf16[12288,64]{0,1:T(8,128)(2,1)S(1)} %copy-done, bf16[6144,240]{1,0:T(8,128)(2,1)S(1)} %bitcast.28, bf16[6144,240]{1,0:T(8,128)(2,1)S(1)} %bitcast.25, bf16[6144,240]{1,0:T(8,128)(2,1)S(1)} %bitcast_negate_fusion), kind=kOutput, calls=%fused_computation.9 | convolution fusion | flops 802160640 | bytes 10543104 | tf_op jit(solution)/shard_map/dot_general | solution.py:68
  167.4 0.8 reshape.80
  (4 shorter events, 0.1 us)
Async XLA Ops:
  6.5 6.8 %copy-start.1 = (f32[96]{0:T(128)S(1)}, f32[96]{0:T(128)}, u32[]{:S(2)}) copy-start(f32[96]{0:T(128)} %param.4) | copy-start | bytes 1156
  6.5 67.5 %all-gather.4.cloned.1.call-start = ((), (), s32[]{:S(2)}) async-start(), calls=%async_computation.2 | async-start | bytes 1769472 | tf_op jit(solution)/shard_map/all_gather | solution.py:30
  31.5 127.0 %all-gather.6.cloned.1.call-start = ((), (), s32[]{:S(2)}) async-start(), calls=%async_computation.3 | async-start | bytes 7864320 | tf_op jit(solution)/shard_map/all_gather | solution.py:30
  162.3 1.4 copy-start
Sparse Core Ops, SparseCore 0:
  31.6 42.3 all-gather.3
  75.8 82.6 all-gather.5
where the time goes:
time: 176 us; the launch traced here: 175 us
  blocking collectives  71.9 us (41%)
  waiting for transfers between devices  66.3 us (38%)
  local copies, waits for them, and re-layouts  17.2 us (10%)
  between operations  14.2 us (8%)
  matrix products  3.7 us (2%)
    all_gather x2, waiting for transfers between devices, all_blocks(): pieces = lax.all_gather(pieces, axes[k], axis=0, tiled=True)  66.2 us
    all_to_all x1, blocking collectives, body(): lax.all_to_all(density, GA, split_axis=2, concat_axis=1, tiled=True)  55.2 us
    all_to_all x1, blocking collectives, from_everyone(): lax.all_to_all(jnp.broadcast_to(x[None], (peers, *x.shape)), axis, 0, 0,...  9.8 us
    all_gather x1, blocking collectives, all_blocks(): pieces = lax.all_gather(pieces, axes[k], axis=0, tiled=True)  6.9 us
    unnamed x5, local copies, waits for them, and re-layouts  6.17 us
    reshape x1, local copies, waits for them, and re-layouts, body(): flattened = columns.reshape(2 * all_g, own_cols)  3.84 us
    dot_general x1, matrix products, body(): lax.dot_general(flattened, stack_left(whole_rows), (((0,), (0,)), ((), ()...  3.7 us
  transfers between devices with their start and end apart: 2, of which 2 were waited for; matrix products, arithmetic and copies ran while one was open for 3% of the time, Pallas kernels for 0%

commit v1 on v0

v1 whole, which is shorter than its diff:
```python
import jax
import jax.numpy as jnp
from jax import lax
from jax.experimental import pallas as pl
from jax.experimental.pallas import tpu as pltpu
from jax.sharding import PartitionSpec as P

MESH = pl.DeviceIdType.MESH
RB = 240
RBP = 256
G = 96
COLS = 4096
WIN = 384
NX, NY, NZ = 4, 2, 8
NA = NX * NY
ORDER = (2, 1, 3, 0)
NCH = len(ORDER)


def place(x, yh, z, yl, c):
    return (yh * (NZ * NX) + z * NX + x, yl * 2 + c)


def kernel(row_ref, coul_ref, dens_ref, out_ref, dv, wpart, s1buf, fbuf, fstack, sbuf, dbuf, zsend, zrecv, own,
           lsem, s1s, s1r, fs, fr, xs, xr, ds, dr, zs, zr):
    ga = lax.axis_index("ga")
    ta = lax.axis_index("ta")
    x, z, yh = ga % NX, (ga // NX) % NZ, ga // (NX * NZ)
    yl, c = ta // 2, ta % 2
    kz, par = z // 2, z % 2

    load = pltpu.make_async_copy(dens_ref, dv, lsem)
    load.start()

    def group(r):
        return place((x + r % NX) % NX, (yh + r // NX) % NY, z, yl, c)

    def along(delta, eps):
        return place(x, yh, 2 * ((kz + delta) % 4) + (par + eps) % 2, yl, c)

    def mates(q):
        return ((yl + q // 2) % 2, (c + q % 2) % 2)

    bar = pltpu.get_barrier_semaphore()
    for r in range(1, NA):
        pl.semaphore_signal(bar, inc=1, device_id=group(r), device_id_type=MESH)
    for s in range(1, NZ):
        pl.semaphore_signal(bar, inc=1, device_id=along(s // 2, s % 2), device_id_type=MESH)
    for q in range(1, 4):
        pl.semaphore_signal(bar, inc=1, device_id=place(x, yh, z, *mates(q)), device_id_type=MESH)

    load.wait()

    start = row_ref[0] * RB - ta * COLS
    tile = jnp.minimum(jnp.maximum(lax.shift_right_arithmetic(start, 7), 0), (COLS - WIN) // 128)
    src = lax.broadcasted_iota(jnp.int32, (WIN, RBP), 0) + tile * 128
    dst = lax.broadcasted_iota(jnp.int32, (WIN, RBP), 1)
    hit = jnp.logical_and(src == dst + start, dst < RB)
    onehot = jnp.where(hit, 1.0, 0.0).astype(jnp.bfloat16)
    weight = jnp.broadcast_to(coul_ref[...], (128, 128)).T[:G, :]
    weight = jnp.concatenate([weight, weight], axis=1)
    for part in range(2):
        window = dv[part, :, :WIN]
        for k in range(1, (COLS - WIN) // 128 + 1):
            window = jnp.where(tile == k, dv[part, :, k * 128:k * 128 + WIN], window)
        picked = jnp.dot(window, onehot, preferred_element_type=jnp.float32)
        wpart[part] = (weight * picked).astype(jnp.bfloat16)

    low = lax.broadcasted_iota(jnp.int32, (G, 128), 1) < 64

    def pack(j):
        zpair = 2 * ((kz + ORDER[j]) % 4)
        z0 = zpair + par
        z1 = zpair + (par + 1) % 2
        for part in range(2):
            for y in range(NY):
                for h in range(2):
                    o0 = pl.multiple_of((y * 16 + z0 * 2 + h) * 128, 128)
                    o1 = pl.multiple_of((y * 16 + z1 * 2 + h) * 128, 128)
                    t0 = dv[part, :, pl.ds(o0, 128)].astype(jnp.float32)
                    t1 = dv[part, :, pl.ds(o1, 128)].astype(jnp.float32)
                    even = jnp.where(low, t0, pltpu.roll(t1, 64, 1))
                    odd = jnp.where(low, pltpu.roll(t0, 64, 1), t1)
                    sbuf[j, y * NX + 2 * h, part * G:(part + 1) * G, :] = even.astype(jnp.bfloat16)
                    sbuf[j, y * NX + 2 * h + 1, part * G:(part + 1) * G, :] = odd.astype(jnp.bfloat16)
        dbuf[j, 0] = sbuf[j, yh * NX + x]

    waits = []

    def send(src, dst, ss, rs, device):
        cp = pltpu.make_async_remote_copy(src_ref=src, dst_ref=dst, send_sem=ss, recv_sem=rs, device_id=device,
                                          device_id_type=MESH)
        cp.start()
        waits.append(cp)
        return cp

    def spread(j):
        got = []
        for r in range(1, NA):
            dest = (yh + r // NX) % NY * NX + (x + r % NX) % NX
            got.append(send(sbuf.at[j, dest], dbuf.at[j, r], ds.at[j, r], dr.at[j, r], group(r)))
        return got

    pack(0)
    pl.semaphore_wait(bar, (NA - 1) + (NZ - 1) + 3)

    first = []
    for q in range(1, 4):
        ylq, cq = mates(q)
        first.append(send(wpart.at[cq], s1buf.at[q - 1], s1s.at[q - 1], s1r.at[q - 1], place(x, yh, z, ylq, cq)))
    arrived = [spread(0)]
    pack(1)
    for cp in first:
        cp.wait_recv()
    total = wpart[c].astype(jnp.float32)
    for q in range(3):
        total = total + s1buf[q].astype(jnp.float32)
    fbuf[0, c] = total.astype(jnp.bfloat16)
    rows = [send(fbuf.at[0, c], fbuf.at[r, c], fs.at[r], fr.at[r], group(r)) for r in range(1, NA)]
    other = place(x, yh, z, yl, (c + 1) % 2)
    across = [send(fbuf.at[0, c], fbuf.at[0, c], xs.at[0], xr.at[0], other)]
    arrived.append(spread(1))
    pack(2)
    arrived.append(spread(2))
    pack(3)
    arrived.append(spread(3))
    for r in range(1, NA):
        rows[r - 1].wait_recv()
        across.append(send(fbuf.at[r, c], fbuf.at[r, c], xs.at[r], xr.at[r], other))
    for r in range(NA):
        across[r].wait_recv()
        re = fbuf[r, 0]
        im = fbuf[r, 1]
        fstack[r * 2 * G:r * 2 * G + G, :RBP] = re
        fstack[r * 2 * G:r * 2 * G + G, RBP:] = -im
        fstack[r * 2 * G + G:(r + 1) * 2 * G, :RBP] = im
        fstack[r * 2 * G + G:(r + 1) * 2 * G, RBP:] = re

    sums = []
    for j in range(NCH):
        for cp in arrived[j]:
            cp.wait_recv()
        cols = dbuf[j].reshape(NA * 2 * G, 128)
        prod = lax.dot_general(cols, fstack[...], (((0,), (0,)), ((), ())), preferred_element_type=jnp.float32)
        for eps in range(2):
            slot = ORDER[j] * 2 + eps
            block = prod[eps * 64:(eps + 1) * 64]
            if slot == 0:
                own[...] = block
            else:
                zsend[slot] = block.astype(jnp.bfloat16)
                sums.append(send(zsend.at[slot], zrecv.at[slot], zs.at[slot], zr.at[slot], along(ORDER[j], eps)))
    acc = own[...]
    for cp, slot in zip(sums, [d * 2 + e for d in ORDER for e in range(2) if d * 2 + e > 0]):
        cp.wait_recv()
        acc = acc + zrecv[slot].astype(jnp.float32)
    out_ref[...] = acc
    for cp in waits:
        cp.wait_send()


def body(density, coulomb, row_block):
    weight = jnp.pad(coulomb.reshape(1, G), ((0, 0), (0, 128 - G)))
    dma = pltpu.SemaphoreType.DMA
    bf16, f32 = jnp.bfloat16, jnp.float32
    out = pl.pallas_call(
        kernel,
        out_shape=jax.ShapeDtypeStruct((64, 2 * RBP), f32),
        in_specs=[
            pl.BlockSpec(memory_space=pltpu.SMEM),
            pl.BlockSpec(memory_space=pltpu.VMEM),
            pl.BlockSpec(memory_space=pl.ANY),
        ],
        out_specs=pl.BlockSpec(memory_space=pltpu.VMEM),
        scratch_shapes=[
            pltpu.VMEM((2, G, COLS), bf16),
            pltpu.VMEM((2, G, RBP), bf16),
            pltpu.VMEM((3, G, RBP), bf16),
            pltpu.VMEM((NA, 2, G, RBP), bf16),
            pltpu.VMEM((NA * 2 * G, 2 * RBP), bf16),
            pltpu.VMEM((NCH, NA, 2 * G, 128), bf16),
            pltpu.VMEM((NCH, NA, 2 * G, 128), bf16),
            pltpu.VMEM((NZ, 64, 2 * RBP), bf16),
            pltpu.VMEM((NZ, 64, 2 * RBP), bf16),
            pltpu.VMEM((64, 2 * RBP), f32),
            dma, dma((3,)), dma((3,)), dma((NA,)), dma((NA,)), dma((NA,)), dma((NA,)),
            dma((NCH, NA)), dma((NCH, NA)), dma((NZ,)), dma((NZ,)),
        ],
        compiler_params=pltpu.CompilerParams(collective_id=0, has_side_effects=True),
        name="exchange",
    )(row_block, weight, density)
    return out.reshape(64, 2, RBP)[:, :, :RB].reshape(1, 64, 2, RB)


def solution(mesh):
    return jax.shard_map(
        body,
        mesh=mesh,
        in_specs=(P(None, "ga", "ta"), P("ga"), P()),
        out_specs=P("ta", "ga", None, None),
        check_vma=False,
    )
```

time: 176 us -> 50.4 us (0.29)
  the two profiles are of different devices: /device:TPU:16 before, /device:TPU:1 now
where the time goes in v1:
time: 50.4 us; the launch traced here: 50.3 us
  Pallas kernels  46.8 us (93%)
  local copies, waits for them, and re-layouts  2.82 us (6%)
  between operations  0.66 us (1%)
    pallas_call x1, Pallas kernels, body(): pl.pallas_call(kernel, out_shape=jax.ShapeDtypeStruct((64, 2 * RBP), f32)...  46.8 us
    reshape x2, local copies, waits for them, and re-layouts, body(): return out.reshape(64, 2, RBP)[:, :, :RB].reshape(1, 64, 2, RB)  1.65 us
    pad x1, local copies, waits for them, and re-layouts, body(): weight = jnp.pad(coulomb.reshape(1, G), ((0, 0), (0, 128 - G)))  1.17 us

profile of v1, /device:TPU:1, one launch (start us, length us, event | category | flops | bytes accessed | tf_op | source)
XLA Modules:
  0.0 50.3 jit_solution(1645490210499423205)
XLA Ops:
  0.7 1.2 %pad.4.coul_ref = f32[1,128]{1,0:T(1,128)} pad(f32[1,96]{1,0:T(1,128)} %bitcast.3, f32[]{:T(128)} %constant.2.clone.1), padding=0_0x0_32 | pad | bytes 900 | tf_op jit(solution)/shard_map/jit(_pad)/pad | solution.py:163
  1.8 46.8 %exchange.1 = f32[64,512]{1,0:T(8,128)} custom-call(s32[1]{0:T(128)S(6)} %copy.4.row_ref, f32[1,128]{1,0:T(1,128)} %pad.4.coul_ref, bf16[2,96,4096]{2,1,0:T(8,128)(2,1)} %dens_ref.1), custom_call_target="tpu_custom_call" | custom-call | tf_op jit(solution)/shard_map/exchange/pallas_call | solution.py:166
  48.6 1.0 %reshape.10 = f32[64,2,256]{2,1,0:T(2,128)S(1)} reshape(f32[64,512]{1,0:T(8,128)} %exchange.1) | data formatting | bytes 262144 | tf_op jit(solution)/shard_map/reshape | solution.py:192
  49.6 0.7 %slice_bitcast_fusion = f32[1,64,2,240]{3,2,1,0:T(2,128)} fusion(f32[64,2,256]{2,1,0:T(2,128)S(1)} %reshape.10), kind=kLoop, calls=%fused_computation | loop fusion | bytes 245760 | tf_op jit(solution)/shard_map/reshape | solution.py:192

commit v2 on v1

v2 whole, which is shorter than its diff:
```python
import jax
import jax.numpy as jnp
from jax import lax
from jax.experimental import pallas as pl
from jax.experimental.pallas import tpu as pltpu
from jax.sharding import PartitionSpec as P

MESH = pl.DeviceIdType.MESH
RB = 240
RBP = 256
G = 96
COLS = 4096
WIN = 384
NX, NY, NZ = 4, 2, 8
ORDER = ((2, 1), (1, 1), (3, 1), (2, 0), (1, 0), (0, 1), (3, 0), (0, 0))
NP = len(ORDER)


def place(x, yh, z, yl, c):
    return (yh * (NZ * NX) + z * NX + x, yl * 2 + c)


def kernel(row_ref, coul_ref, dens_ref, out_ref, dv, wpart, s1buf, fbuf, fstack, sbuf, dbuf, ysend, yrecv, zsend, zrecv, own,
           lsem, s1s, s1r, fs, fr, xs, xr, ds, dr, ys, yr, zs, zr):
    ga = lax.axis_index("ga")
    ta = lax.axis_index("ta")
    x, z, yh = ga % NX, (ga // NX) % NZ, ga // (NX * NZ)
    yl, c = ta // 2, ta % 2
    kz, par = z // 2, z % 2
    other = (yh + 1) % 2

    load = pltpu.make_async_copy(dens_ref, dv, lsem)
    load.start()

    def beside(r):
        return place((x + r) % NX, yh, z, yl, c)

    def along(delta, eps):
        return place(x, yh, 2 * ((kz + delta) % 4) + (par + eps) % 2, yl, c)

    def mates(q):
        return ((yl + q // 2) % 2, (c + q % 2) % 2)

    opposite = place(x, other, z, yl, c)
    twin = place(x, yh, z, yl, (c + 1) % 2)

    bar = pltpu.get_barrier_semaphore()
    peers = [beside(r) for r in range(1, NX)] + [opposite] + [along(s // 2, s % 2) for s in range(1, NZ)]
    peers += [place(x, yh, z, *mates(q)) for q in range(1, 4)]
    for peer in peers:
        pl.semaphore_signal(bar, inc=1, device_id=peer, device_id_type=MESH)

    with jax.named_scope("load_wait"):
        load.wait()

    start = row_ref[0] * RB - ta * COLS
    tile = jnp.minimum(jnp.maximum(lax.shift_right_arithmetic(start, 7), 0), (COLS - WIN) // 128)
    src = lax.broadcasted_iota(jnp.int32, (WIN, RBP), 0) + tile * 128
    dst = lax.broadcasted_iota(jnp.int32, (WIN, RBP), 1)
    hit = jnp.logical_and(src == dst + start, dst < RB)
    onehot = jnp.where(hit, 1.0, 0.0).astype(jnp.bfloat16)
    diag = lax.broadcasted_iota(jnp.int32, (G, G), 0) == lax.broadcasted_iota(jnp.int32, (G, G), 1)
    weight = jnp.sum(jnp.where(diag, jnp.broadcast_to(coul_ref[...], (G, G)), 0.0), axis=1, keepdims=True)
    for part in range(2):
        window = dv[part, :, :WIN]
        for k in range(1, (COLS - WIN) // 128 + 1):
            window = jnp.where(tile == k, dv[part, :, k * 128:k * 128 + WIN], window)
        picked = jnp.dot(window, onehot, preferred_element_type=jnp.float32)
        wpart[part] = (weight * picked).astype(jnp.bfloat16)

    low = lax.broadcasted_iota(jnp.int32, (G, 128), 1) < 64

    def pack(p):
        delta, w = ORDER[p]
        y = (yh + w) % NY
        zpair = 2 * ((kz + delta) % 4)
        z0 = zpair + par
        z1 = zpair + (par + 1) % 2
        for part in range(2):
            for h in range(2):
                o0 = pl.multiple_of((y * 16 + z0 * 2 + h) * 128, 128)
                o1 = pl.multiple_of((y * 16 + z1 * 2 + h) * 128, 128)
                t0 = dv[part, :, pl.ds(o0, 128)].astype(jnp.float32)
                t1 = dv[part, :, pl.ds(o1, 128)].astype(jnp.float32)
                even = jnp.where(low, t0, pltpu.roll(t1, 64, 1))
                odd = jnp.where(low, pltpu.roll(t0, 64, 1), t1)
                sbuf[p, 2 * h, part * G:(part + 1) * G, :] = even.astype(jnp.bfloat16)
                sbuf[p, 2 * h + 1, part * G:(part + 1) * G, :] = odd.astype(jnp.bfloat16)
        dbuf[p, 0] = sbuf[p, x]

    waits = []

    def send(src, dst, ss, rs, device):
        cp = pltpu.make_async_remote_copy(src_ref=src, dst_ref=dst, send_sem=ss, recv_sem=rs, device_id=device,
                                          device_id_type=MESH)
        cp.start()
        waits.append(cp)
        return cp

    def spread(p):
        return [send(sbuf.at[p, (x + r) % NX], dbuf.at[p, r], ds.at[p, r], dr.at[p, r], beside(r)) for r in range(1, NX)]

    with jax.named_scope("pack0"):
        pack(0)
    with jax.named_scope("bar_wait"):
        pl.semaphore_wait(bar, len(peers))

    first = []
    for q in range(1, 4):
        ylq, cq = mates(q)
        first.append(send(wpart.at[cq], s1buf.at[q - 1], s1s.at[q - 1], s1r.at[q - 1], place(x, yh, z, ylq, cq)))
    arrived = [spread(0)]
    with jax.named_scope("pack1"):
        pack(1)
        pack(2)
    with jax.named_scope("s1_wait"):
        for cp in first:
            cp.wait_recv()
    total = wpart[c].astype(jnp.float32)
    for q in range(3):
        total = total + s1buf[q].astype(jnp.float32)
    fbuf[0, c] = total.astype(jnp.bfloat16)
    rows = [send(fbuf.at[0, c], fbuf.at[r, c], fs.at[r], fr.at[r], beside(r)) for r in range(1, NX)]
    across = [send(fbuf.at[0, c], fbuf.at[0, c], xs.at[0], xr.at[0], twin)]
    arrived.append(spread(1))
    arrived.append(spread(2))
    with jax.named_scope("packs"):
        for p in range(3, NP):
            pack(p)
            arrived.append(spread(p))
    for r in range(1, NX):
        with jax.named_scope(f"rows_wait{r}"):
            rows[r - 1].wait_recv()
        across.append(send(fbuf.at[r, c], fbuf.at[r, c], xs.at[r], xr.at[r], twin))
    for r in range(NX):
        with jax.named_scope(f"across_wait{r}"):
            across[r].wait_recv()
        re = fbuf[r, 0]
        im = fbuf[r, 1]
        fstack[r * 2 * G:r * 2 * G + G, :RBP] = re
        fstack[r * 2 * G:r * 2 * G + G, RBP:] = -im
        fstack[r * 2 * G + G:(r + 1) * 2 * G, :RBP] = im
        fstack[r * 2 * G + G:(r + 1) * 2 * G, RBP:] = re

    halves = {}
    sums = []
    for p, (delta, w) in enumerate(ORDER):
        with jax.named_scope(f"piece_wait{p}"):
            for cp in arrived[p]:
                cp.wait_recv()
        cols = dbuf[p].reshape(NX * 2 * G, 128)
        prod = lax.dot_general(cols, fstack[...], (((0,), (0,)), ((), ())), preferred_element_type=jnp.float32)
        if w:
            ysend[delta] = prod.astype(jnp.bfloat16)
            halves[delta] = send(ysend.at[delta], yrecv.at[delta], ys.at[delta], yr.at[delta], opposite)
        else:
            with jax.named_scope(f"half_wait{p}"):
                halves[delta].wait_recv()
            both = prod + yrecv[delta].astype(jnp.float32)
            for eps in range(2):
                slot = delta * 2 + eps
                block = both[eps * 64:(eps + 1) * 64]
                if slot == 0:
                    own[...] = block
                else:
                    zsend[slot] = block.astype(jnp.bfloat16)
                    cp = send(zsend.at[slot], zrecv.at[slot], zs.at[slot], zr.at[slot], along(delta, eps))
                    sums.append((cp, slot))
    acc = own[...]
    for cp, slot in sums:
        with jax.named_scope(f"zwait{slot}"):
            cp.wait_recv()
        acc = acc + zrecv[slot].astype(jnp.float32)
    out_ref[:, 0, :] = acc[:, :RB]
    out_ref[:, 1, :] = acc[:, RBP:RBP + RB]
    with jax.named_scope("send_waits"):
        for cp in waits:
            cp.wait_send()


def body(density, coulomb, row_block):
    dma = pltpu.SemaphoreType.DMA
    bf16, f32 = jnp.bfloat16, jnp.float32
    out = pl.pallas_call(
        kernel,
        out_shape=jax.ShapeDtypeStruct((64, 2, RB), f32),
        in_specs=[
            pl.BlockSpec(memory_space=pltpu.SMEM),
            pl.BlockSpec(memory_space=pltpu.VMEM),
            pl.BlockSpec(memory_space=pl.ANY),
        ],
        out_specs=pl.BlockSpec(memory_space=pltpu.VMEM),
        scratch_shapes=[
            pltpu.VMEM((2, G, COLS), bf16),
            pltpu.VMEM((2, G, RBP), bf16),
            pltpu.VMEM((3, G, RBP), bf16),
            pltpu.VMEM((NX, 2, G, RBP), bf16),
            pltpu.VMEM((NX * 2 * G, 2 * RBP), bf16),
            pltpu.VMEM((NP, NX, 2 * G, 128), bf16),
            pltpu.VMEM((NP, NX, 2 * G, 128), bf16),
            pltpu.VMEM((4, 128, 2 * RBP), bf16),
            pltpu.VMEM((4, 128, 2 * RBP), bf16),
            pltpu.VMEM((NZ, 64, 2 * RBP), bf16),
            pltpu.VMEM((NZ, 64, 2 * RBP), bf16),
            pltpu.VMEM((64, 2 * RBP), f32),
            dma, dma((3,)), dma((3,)), dma((NX,)), dma((NX,)), dma((NX,)), dma((NX,)),
            dma((NP, NX)), dma((NP, NX)), dma((4,)), dma((4,)), dma((NZ,)), dma((NZ,)),
        ],
        compiler_params=pltpu.CompilerParams(collective_id=0, has_side_effects=True),
        name="exchange",
    )(row_block, coulomb.reshape(1, G), density)
    return out.reshape(1, 64, 2, RB)


def solution(mesh):
    return jax.shard_map(
        body,
        mesh=mesh,
        in_specs=(P(None, "ga", "ta"), P("ga"), P()),
        out_specs=P("ta", "ga", None, None),
        check_vma=False,
    )
```

time: 50.4 us -> 45.9 us (0.911)
  Pallas kernels: 46.8 us -> 43.6 us
  local copies, waits for them, and re-layouts: 2.82 us -> 1.57 us
    pallas_call x1, Pallas kernels: 46.8 us -> 43.6 us  [body(): pl.pallas_call(kernel, out_shape=jax.ShapeDtypeStruct((64, 2, RB), f32),...]
    reshape x2 -> x0, local copies, waits for them, and re-layouts: 1.65 us -> none  [body(): return out.reshape(64, 2, RBP)[:, :, :RB].reshape(1, 64, 2, RB)]
    unnamed x0 -> x1, local copies, waits for them, and re-layouts: none -> 1.57 us
    pad x1 -> x0, local copies, waits for them, and re-layouts: 1.17 us -> none  [body(): weight = jnp.pad(coulomb.reshape(1, G), ((0, 0), (0, 128 - G)))]
where the time goes in v2:
time: 45.9 us; the launch traced here: 45.8 us
  Pallas kernels  43.6 us (95%)
  local copies, waits for them, and re-layouts  1.57 us (3%)
  between operations  0.66 us (1%)
    pallas_call x1, Pallas kernels, body(): pl.pallas_call(kernel, out_shape=jax.ShapeDtypeStruct((64, 2, RB), f32),...  43.6 us
    unnamed x1, local copies, waits for them, and re-layouts  1.57 us

profile of v2, /device:TPU:1, one launch (start us, length us, event | category | flops | bytes accessed | tf_op | source)
XLA Modules:
  0.0 45.8 jit_solution(3059117463112294086)
XLA Ops:
  0.7 43.6 %exchange.1 = f32[64,2,240]{2,1,0:T(2,128)} custom-call(s32[1]{0:T(128)S(6)} %copy.5.row_ref, f32[1,96]{1,0:T(1,128)} %bitcast.3, bf16[2,96,4096]{2,1,0:T(8,128)(2,1)} %dens_ref.1), custom_call_target="tpu_custom_call" | custom-call | tf_op jit(solution)/shard_map/exchange/pallas_call | solution.py:184
  44.2 1.6 %copy.6 = f32[1,64,2,240]{3,2,1,0:T(2,128)} copy(f32[1,64,2,240]{3,2,1,0:T(2,128)} %bitcast.2) | data formatting | bytes 245760

commit v3 on v2

--- a/solution.py
+++ b/solution.py
@@ -12,7 +12,7 @@
 COLS = 4096
 WIN = 384
 NX, NY, NZ = 4, 2, 8
-ORDER = ((2, 1), (1, 1), (3, 1), (2, 0), (1, 0), (0, 1), (3, 0), (0, 0))
+ORDER = ((2, 1), (3, 1), (1, 1), (2, 0), (0, 1), (3, 0), (1, 0), (0, 0))
 NP = len(ORDER)
 
 
@@ -20,8 +20,8 @@
     return (yh * (NZ * NX) + z * NX + x, yl * 2 + c)
 
 
-def kernel(row_ref, coul_ref, dens_ref, out_ref, dv, wpart, s1buf, fbuf, fstack, sbuf, dbuf, ysend, yrecv, zsend, zrecv, own,
-           lsem, s1s, s1r, fs, fr, xs, xr, ds, dr, ys, yr, zs, zr):
+def kernel(row_hbm, coul_hbm, dens_ref, out_ref, row_ref, coul_ref, dv, wpart, s1buf, fbuf, fstack, sbuf, dbuf, ysend, yrecv, zsend, zrecv, own,
+           lsem, ready, s1s, s1r, fs, fr, xs, xr, ds, dr, ys, yr, zs, zr):
     ga = lax.axis_index("ga")
     ta = lax.axis_index("ta")
     x, z, yh = ga % NX, (ga // NX) % NZ, ga // (NX * NZ)
@@ -29,14 +29,20 @@
     kz, par = z // 2, z % 2
     other = (yh + 1) % 2
 
-    load = pltpu.make_async_copy(dens_ref, dv, lsem)
-    load.start()
+    loads = [pltpu.make_async_copy(a, b, lsem.at[i])
+             for i, (a, b) in enumerate(((dens_ref, dv), (row_hbm, row_ref), (coul_hbm, coul_ref)))]
+    for load in loads:
+        load.start()
+
+    def pair(m):
+        a, b = kz // 2, kz % 2
+        return (a + m // 2) % 2 * 2 + (b + m % 2) % 2
 
     def beside(r):
         return place((x + r) % NX, yh, z, yl, c)
 
     def along(delta, eps):
-        return place(x, yh, 2 * ((kz + delta) % 4) + (par + eps) % 2, yl, c)
+        return place(x, yh, 2 * pair(delta) + (par + eps) % 2, yl, c)
 
     def mates(q):
         return ((yl + q // 2) % 2, (c + q % 2) % 2)
@@ -45,13 +51,28 @@
     twin = place(x, yh, z, yl, (c + 1) % 2)
 
     bar = pltpu.get_barrier_semaphore()
-    peers = [beside(r) for r in range(1, NX)] + [opposite] + [along(s // 2, s % 2) for s in range(1, NZ)]
+    peers = [beside(r) for r in range(1, NX)] + [opposite]
     peers += [place(x, yh, z, *mates(q)) for q in range(1, 4)]
     for peer in peers:
         pl.semaphore_signal(bar, inc=1, device_id=peer, device_id_type=MESH)
 
+    def greet(sem, d):
+        @pl.when(z + d < NZ)
+        def _():
+            pl.semaphore_signal(sem, inc=1, device_id=place(x, yh, z + d, yl, c), device_id_type=MESH)
+
+        @pl.when(z >= d)
+        def _():
+            pl.semaphore_signal(sem, inc=1, device_id=place(x, yh, z - d, yl, c), device_id_type=MESH)
+
+    def met(d):
+        return jnp.where(z + d < NZ, 1, 0) + jnp.where(z >= d, 1, 0)
+
+    greet(bar, 1)
+
     with jax.named_scope("load_wait"):
-        load.wait()
+        for load in loads:
+            load.wait()
 
     start = row_ref[0] * RB - ta * COLS
     tile = jnp.minimum(jnp.maximum(lax.shift_right_arithmetic(start, 7), 0), (COLS - WIN) // 128)
@@ -73,7 +94,7 @@
     def pack(p):
         delta, w = ORDER[p]
         y = (yh + w) % NY
-        zpair = 2 * ((kz + delta) % 4)
+        zpair = 2 * pair(delta)
         z0 = zpair + par
         z1 = zpair + (par + 1) % 2
         for part in range(2):
@@ -103,16 +124,20 @@
     with jax.named_scope("pack0"):
         pack(0)
     with jax.named_scope("bar_wait"):
-        pl.semaphore_wait(bar, len(peers))
+        pl.semaphore_wait(bar, len(peers) + met(1))
 
     first = []
     for q in range(1, 4):
         ylq, cq = mates(q)
         first.append(send(wpart.at[cq], s1buf.at[q - 1], s1s.at[q - 1], s1r.at[q - 1], place(x, yh, z, ylq, cq)))
     arrived = [spread(0)]
-    with jax.named_scope("pack1"):
-        pack(1)
-        pack(2)
+    greet(ready.at[0], 1)
+    with jax.named_scope("packs"):
+        for p in range(1, NP):
+            pack(p)
+    with jax.named_scope("ready0"):
+        pl.semaphore_wait(ready.at[0], met(1))
+    greet(ready.at[1], 2)
     with jax.named_scope("s1_wait"):
         for cp in first:
             cp.wait_recv()
@@ -121,13 +146,16 @@
         total = total + s1buf[q].astype(jnp.float32)
     fbuf[0, c] = total.astype(jnp.bfloat16)
     rows = [send(fbuf.at[0, c], fbuf.at[r, c], fs.at[r], fr.at[r], beside(r)) for r in range(1, NX)]
+    del waits[-len(rows):]
     across = [send(fbuf.at[0, c], fbuf.at[0, c], xs.at[0], xr.at[0], twin)]
-    arrived.append(spread(1))
-    arrived.append(spread(2))
-    with jax.named_scope("packs"):
-        for p in range(3, NP):
-            pack(p)
-            arrived.append(spread(p))
+    with jax.named_scope("rows_sent"):
+        for cp in rows:
+            cp.wait_send()
+    for p in range(1, NP):
+        arrived.append(spread(p))
+    with jax.named_scope("ready1"):
+        pl.semaphore_wait(ready.at[1], met(2))
+    greet(ready.at[2], 4)
     for r in range(1, NX):
         with jax.named_scope(f"rows_wait{r}"):
             rows[r - 1].wait_recv()
@@ -144,6 +172,7 @@
 
     halves = {}
     sums = []
+    greeted = False
     for p, (delta, w) in enumerate(ORDER):
         with jax.named_scope(f"piece_wait{p}"):
             for cp in arrived[p]:
@@ -156,6 +185,10 @@
         else:
             with jax.named_scope(f"half_wait{p}"):
                 halves[delta].wait_recv()
+            if not greeted:
+                greeted = True
+                with jax.named_scope("ready2"):
+                    pl.semaphore_wait(ready.at[2], met(4))
             both = prod + yrecv[delta].astype(jnp.float32)
             for eps in range(2):
                 slot = delta * 2 + eps
@@ -183,14 +216,12 @@
     bf16, f32 = jnp.bfloat16, jnp.float32
     out = pl.pallas_call(
         kernel,
-        out_shape=jax.ShapeDtypeStruct((64, 2, RB), f32),
-        in_specs=[
-            pl.BlockSpec(memory_space=pltpu.SMEM),
-            pl.BlockSpec(memory_space=pltpu.VMEM),
-            pl.BlockSpec(memory_space=pl.ANY),
-        ],
+        out_shape=pltpu.VMEM((64, 2, RB), f32),
+        in_specs=[pl.BlockSpec(memory_space=pltpu.HBM)] * 3,
         out_specs=pl.BlockSpec(memory_space=pltpu.VMEM),
         scratch_shapes=[
+            pltpu.SMEM((1,), jnp.int32),
+            pltpu.VMEM((1, G), f32),
             pltpu.VMEM((2, G, COLS), bf16),
             pltpu.VMEM((2, G, RBP), bf16),
             pltpu.VMEM((3, G, RBP), bf16),
@@ -203,7 +234,7 @@
             pltpu.VMEM((NZ, 64, 2 * RBP), bf16),
             pltpu.VMEM((NZ, 64, 2 * RBP), bf16),
             pltpu.VMEM((64, 2 * RBP), f32),
-            dma, dma((3,)), dma((3,)), dma((NX,)), dma((NX,)), dma((NX,)), dma((NX,)),
+            dma((3,)), pltpu.SemaphoreType.REGULAR((3,)), dma((3,)), dma((3,)), dma((NX,)), dma((NX,)), dma((NX,)), dma((NX,)),
             dma((NP, NX)), dma((NP, NX)), dma((4,)), dma((4,)), dma((NZ,)), dma((NZ,)),
         ],
         compiler_params=pltpu.CompilerParams(collective_id=0, has_side_effects=True),

time: 45.9 us -> 43.4 us (0.946)
  Pallas kernels: 43.6 us -> 42 us
  local copies, waits for them, and re-layouts: 1.57 us -> 0.66 us
    pallas_call x1, Pallas kernels: 43.6 us -> 42 us  [body(): pl.pallas_call(kernel, out_shape=pltpu.VMEM((64, 2, RB), f32), in_specs=[...]
    unnamed x1, local copies, waits for them, and re-layouts: 1.57 us -> 0.66 us
where the time goes in v3:
time: 43.4 us; the launch traced here: 43.3 us
  Pallas kernels  42 us (97%)
  local copies, waits for them, and re-layouts  0.66 us (2%)
  between operations  0.66 us (2%)
    pallas_call x1, Pallas kernels, body(): pl.pallas_call(kernel, out_shape=pltpu.VMEM((64, 2, RB), f32), in_specs=[...  42 us

profile of v3, /device:TPU:1, one launch (start us, length us, event | category | flops | bytes accessed | tf_op | source)
XLA Modules:
  0.0 43.3 jit_solution(14091261743458412411)
XLA Ops:
  0.7 42.0 %exchange.1 = f32[64,2,240]{2,1,0:T(2,128)S(1)} custom-call(s32[1]{0:T(128)S(6)} %copy.6.row_hbm, f32[1,96]{1,0:T(1,128)} %bitcast.3, bf16[2,96,4096]{2,1,0:T(8,128)(2,1)} %dens_ref.1), custom_call_target="tpu_custom_call" | custom-call | tf_op jit(solution)/shard_map/exchange/pallas_call | solution.py:217
  42.6 0.7 %copy.5 = f32[1,64,2,240]{3,2,1,0:T(2,128)} copy(f32[1,64,2,240]{3,2,1,0:T(2,128)S(1)} %bitcast.2) | data formatting | bytes 245760

commit v4 on v3

--- a/solution.py
+++ b/solution.py
@@ -12,7 +12,8 @@
 COLS = 4096
 WIN = 384
 NX, NY, NZ = 4, 2, 8
-ORDER = ((2, 1), (3, 1), (1, 1), (2, 0), (0, 1), (3, 0), (1, 0), (0, 0))
+Q = 48
+ORDER = ((2, 1), (3, 1), (2, 0), (1, 1), (3, 0), (0, 1), (1, 0), (0, 0))
 NP = len(ORDER)
 
 
@@ -51,8 +52,8 @@
     twin = place(x, yh, z, yl, (c + 1) % 2)
 
     bar = pltpu.get_barrier_semaphore()
-    peers = [beside(r) for r in range(1, NX)] + [opposite]
-    peers += [place(x, yh, z, *mates(q)) for q in range(1, 4)]
+    peers = [opposite] + [place(x, yh, z, *mates(q)) for q in range(1, 4)]
+    peers += [place((x + r) % NX, yh, z, (yl + u) % 2, c) for r in range(1, NX) for u in range(2)]
     for peer in peers:
         pl.semaphore_signal(bar, inc=1, device_id=peer, device_id_type=MESH)
 
@@ -87,7 +88,9 @@
         for k in range(1, (COLS - WIN) // 128 + 1):
             window = jnp.where(tile == k, dv[part, :, k * 128:k * 128 + WIN], window)
         picked = jnp.dot(window, onehot, preferred_element_type=jnp.float32)
-        wpart[part] = (weight * picked).astype(jnp.bfloat16)
+        weighted = (weight * picked).astype(jnp.bfloat16)
+        wpart[2 * part] = weighted[:Q]
+        wpart[2 * part + 1] = weighted[Q:]
 
     low = lax.broadcasted_iota(jnp.int32, (G, 128), 1) < 64
 
@@ -129,7 +132,7 @@
     first = []
     for q in range(1, 4):
         ylq, cq = mates(q)
-        first.append(send(wpart.at[cq], s1buf.at[q - 1], s1s.at[q - 1], s1r.at[q - 1], place(x, yh, z, ylq, cq)))
+        first.append(send(wpart.at[ylq * 2 + cq], s1buf.at[q - 1], s1s.at[q - 1], s1r.at[q - 1], place(x, yh, z, ylq, cq)))
     arrived = [spread(0)]
     greet(ready.at[0], 1)
     with jax.named_scope("packs"):
@@ -141,30 +144,33 @@
     with jax.named_scope("s1_wait"):
         for cp in first:
             cp.wait_recv()
-    total = wpart[c].astype(jnp.float32)
+    total = wpart[ta].astype(jnp.float32)
     for q in range(3):
         total = total + s1buf[q].astype(jnp.float32)
-    fbuf[0, c] = total.astype(jnp.bfloat16)
-    rows = [send(fbuf.at[0, c], fbuf.at[r, c], fs.at[r], fr.at[r], beside(r)) for r in range(1, NX)]
-    del waits[-len(rows):]
-    across = [send(fbuf.at[0, c], fbuf.at[0, c], xs.at[0], xr.at[0], twin)]
-    with jax.named_scope("rows_sent"):
-        for cp in rows:
-            cp.wait_send()
+    fbuf[0, ta] = total.astype(jnp.bfloat16)
+    rows, across = [None], []
+    for n in range(1, 2 * NX):
+        r, u = n // 2, n % 2
+        dest = place((x + r) % NX, yh, z, (yl + u) % 2, c)
+        rows.append(send(fbuf.at[0, ta], fbuf.at[r, ta], fs.at[n], fr.at[n], dest))
+    across.append(send(fbuf.at[0, ta], fbuf.at[0, ta], xs.at[0], xr.at[0], twin))
     for p in range(1, NP):
         arrived.append(spread(p))
     with jax.named_scope("ready1"):
         pl.semaphore_wait(ready.at[1], met(2))
     greet(ready.at[2], 4)
-    for r in range(1, NX):
-        with jax.named_scope(f"rows_wait{r}"):
-            rows[r - 1].wait_recv()
-        across.append(send(fbuf.at[r, c], fbuf.at[r, c], xs.at[r], xr.at[r], twin))
+    for n in range(1, 2 * NX):
+        r, u = n // 2, n % 2
+        with jax.named_scope(f"rows_wait{n}"):
+            rows[n].wait_recv()
+        part = fbuf.at[r, (yl + u) % 2 * 2 + c]
+        across.append(send(part, part, xs.at[n], xr.at[n], twin))
     for r in range(NX):
         with jax.named_scope(f"across_wait{r}"):
-            across[r].wait_recv()
-        re = fbuf[r, 0]
-        im = fbuf[r, 1]
+            across[2 * r].wait_recv()
+            across[2 * r + 1].wait_recv()
+        re = fbuf[r, 0:2].reshape(G, RBP)
+        im = fbuf[r, 2:4].reshape(G, RBP)
         fstack[r * 2 * G:r * 2 * G + G, :RBP] = re
         fstack[r * 2 * G:r * 2 * G + G, RBP:] = -im
         fstack[r * 2 * G + G:(r + 1) * 2 * G, :RBP] = im
@@ -181,18 +187,21 @@
         prod = lax.dot_general(cols, fstack[...], (((0,), (0,)), ((), ())), preferred_element_type=jnp.float32)
         if w:
             ysend[delta] = prod.astype(jnp.bfloat16)
-            halves[delta] = send(ysend.at[delta], yrecv.at[delta], ys.at[delta], yr.at[delta], opposite)
+            for eps in range(2):
+                part = pl.ds(eps * 64, 64)
+                halves[delta, eps] = send(ysend.at[delta, part], yrecv.at[delta, part], ys.at[2 * delta + eps],
+                                          yr.at[2 * delta + eps], opposite)
         else:
-            with jax.named_scope(f"half_wait{p}"):
-                halves[delta].wait_recv()
             if not greeted:
                 greeted = True
                 with jax.named_scope("ready2"):
                     pl.semaphore_wait(ready.at[2], met(4))
-            both = prod + yrecv[delta].astype(jnp.float32)
             for eps in range(2):
                 slot = delta * 2 + eps
-                block = both[eps * 64:(eps + 1) * 64]
+                with jax.named_scope(f"half_wait{p}{eps}"):
+                    halves[delta, eps].wait_recv()
+                part = slice(eps * 64, (eps + 1) * 64)
+                block = prod[part] + yrecv[delta, part].astype(jnp.float32)
                 if slot == 0:
                     own[...] = block
                 else:
@@ -223,9 +232,9 @@
             pltpu.SMEM((1,), jnp.int32),
             pltpu.VMEM((1, G), f32),
             pltpu.VMEM((2, G, COLS), bf16),
-            pltpu.VMEM((2, G, RBP), bf16),
-            pltpu.VMEM((3, G, RBP), bf16),
-            pltpu.VMEM((NX, 2, G, RBP), bf16),
+            pltpu.VMEM((4, Q, RBP), bf16),
+            pltpu.VMEM((3, Q, RBP), bf16),
+            pltpu.VMEM((NX, 4, Q, RBP), bf16),
             pltpu.VMEM((NX * 2 * G, 2 * RBP), bf16),
             pltpu.VMEM((NP, NX, 2 * G, 128), bf16),
             pltpu.VMEM((NP, NX, 2 * G, 128), bf16),
@@ -234,8 +243,8 @@
             pltpu.VMEM((NZ, 64, 2 * RBP), bf16),
             pltpu.VMEM((NZ, 64, 2 * RBP), bf16),
             pltpu.VMEM((64, 2 * RBP), f32),
-            dma((3,)), pltpu.SemaphoreType.REGULAR((3,)), dma((3,)), dma((3,)), dma((NX,)), dma((NX,)), dma((NX,)), dma((NX,)),
-            dma((NP, NX)), dma((NP, NX)), dma((4,)), dma((4,)), dma((NZ,)), dma((NZ,)),
+            dma((3,)), pltpu.SemaphoreType.REGULAR((3,)), dma((3,)), dma((3,)), dma((2 * NX,)), dma((2 * NX,)), dma((2 * NX,)), dma((2 * NX,)),
+            dma((NP, NX)), dma((NP, NX)), dma((NZ,)), dma((NZ,)), dma((NZ,)), dma((NZ,)),
         ],
         compiler_params=pltpu.CompilerParams(collective_id=0, has_side_effects=True),
         name="exchange",

time: 43.4 us -> 41.1 us (0.947)
  the two profiles are of different devices: /device:TPU:1 before, /device:TPU:16 now
where the time goes in v4:
time: 41.1 us; the launch traced here: 41 us
  Pallas kernels  39.7 us (97%)
  local copies, waits for them, and re-layouts  0.66 us (2%)
  between operations  0.66 us (2%)
    pallas_call x1, Pallas kernels, body(): pl.pallas_call(kernel, out_shape=pltpu.VMEM((64, 2, RB), f32), in_specs=[...  39.7 us

profile of v4, /device:TPU:16, one launch (start us, length us, event | category | flops | bytes accessed | tf_op | source)
XLA Modules:
  0.0 41.0 jit_solution(15542655422437545420)
XLA Ops:
  0.7 39.7 %exchange.1 = f32[64,2,240]{2,1,0:T(2,128)S(1)} custom-call(s32[1]{0:T(128)S(6)} %copy.6.row_hbm, f32[1,96]{1,0:T(1,128)} %bitcast.3, bf16[2,96,4096]{2,1,0:T(8,128)(2,1)} %dens_ref.1), custom_call_target="tpu_custom_call" | custom-call | tf_op jit(solution)/shard_map/exchange/pallas_call | solution.py:226
  40.3 0.7 %copy.5 = f32[1,64,2,240]{3,2,1,0:T(2,128)} copy(f32[1,64,2,240]{3,2,1,0:T(2,128)S(1)} %bitcast.2) | data formatting | bytes 245760

commit v5 on v4

v5 whole, which is shorter than its diff:
```python
import jax
import jax.numpy as jnp
from jax import lax
from jax.experimental import pallas as pl
from jax.experimental.pallas import tpu as pltpu
from jax.sharding import PartitionSpec as P

MESH = pl.DeviceIdType.MESH
RB = 240
RBP = 256
G = 96
COLS = 4096
WIN = 384
NX, NY, NZ = 4, 2, 8
Q = 48
ORDER = ((2, 1), (2, 0), (3, 1), (1, 1), (3, 0), (1, 0), (0, 1), (0, 0))
NP = len(ORDER)
SUMS = {4: (2,), 5: (3,), 6: (1,), 7: (0,)}
EARLY = 1


def place(x, yh, z, yl, c):
    return (yh * (NZ * NX) + z * NX + x, yl * 2 + c)


def kernel(row_hbm, coul_hbm, dens_ref, out_ref, row_ref, coul_ref, dv, wpart, s1buf, fbuf, spare, fstack, sbuf, dbuf, csend, crecv, keep, zsend, zrecv,
           lsem, ready, s1s, s1r, fs, fr, ts, tr, ds, dr, cs, cr, zs, zr):
    ga = lax.axis_index("ga")
    ta = lax.axis_index("ta")
    x, z, yh = ga % NX, (ga // NX) % NZ, ga // (NX * NZ)
    yl, c = ta // 2, ta % 2
    kz, par = z // 2, z % 2

    loads = [pltpu.make_async_copy(a, b, lsem.at[i])
             for i, (a, b) in enumerate(((dens_ref, dv), (row_hbm, row_ref), (coul_hbm, coul_ref)))]
    for load in loads:
        load.start()

    def pair(m):
        a, b = kz // 2, kz % 2
        return (a + m // 2) % 2 * 2 + (b + m % 2) % 2

    def beside(r):
        return place((x + r) % NX, yh, z, yl, c)

    def along(m):
        return place(x, yh, 2 * pair(m) + par, yl, c)

    def square(e):
        return place(x, (yh + e // 2) % NY, 2 * kz + (par + e % 2) % 2, yl, c)

    def mates(q):
        return ((yl + q // 2) % 2, (c + q % 2) % 2)

    twin = place(x, yh, z, yl, (c + 1) % 2)

    bar = pltpu.get_barrier_semaphore()
    peers = [square(2), square(3)] + [place(x, yh, z, *mates(q)) for q in range(1, 4)]
    peers += [place((x + r) % NX, yh, z, (yl + u) % 2, c) for r in range(1, NX) for u in range(2)]
    for peer in peers:
        pl.semaphore_signal(bar, inc=1, device_id=peer, device_id_type=MESH)

    def greet(sem, d):
        @pl.when(z + d < NZ)
        def _():
            pl.semaphore_signal(sem, inc=1, device_id=place(x, yh, z + d, yl, c), device_id_type=MESH)

        @pl.when(z >= d)
        def _():
            pl.semaphore_signal(sem, inc=1, device_id=place(x, yh, z - d, yl, c), device_id_type=MESH)

    def met(d):
        return jnp.where(z + d < NZ, 1, 0) + jnp.where(z >= d, 1, 0)

    greet(bar, 1)

    with jax.named_scope("load_wait"):
        for load in loads:
            load.wait()

    start = row_ref[0] * RB - ta * COLS
    tile = jnp.minimum(jnp.maximum(lax.shift_right_arithmetic(start, 7), 0), (COLS - WIN) // 128)
    src = lax.broadcasted_iota(jnp.int32, (WIN, RBP), 0) + tile * 128
    dst = lax.broadcasted_iota(jnp.int32, (WIN, RBP), 1)
    hit = jnp.logical_and(src == dst + start, dst < RB)
    onehot = jnp.where(hit, 1.0, 0.0).astype(jnp.bfloat16)
    diag = lax.broadcasted_iota(jnp.int32, (G, G), 0) == lax.broadcasted_iota(jnp.int32, (G, G), 1)
    weight = jnp.sum(jnp.where(diag, jnp.broadcast_to(coul_ref[...], (G, G)), 0.0), axis=1, keepdims=True)
    for part in range(2):
        window = dv[part, :, :WIN]
        for k in range(1, (COLS - WIN) // 128 + 1):
            window = jnp.where(tile == k, dv[part, :, k * 128:k * 128 + WIN], window)
        picked = jnp.dot(window, onehot, preferred_element_type=jnp.float32)
        weighted = (weight * picked).astype(jnp.bfloat16)
        wpart[2 * part] = weighted[:Q]
        wpart[2 * part + 1] = weighted[Q:]

    low = lax.broadcasted_iota(jnp.int32, (G, 128), 1) < 64

    def pack(p):
        delta, w = ORDER[p]
        y = (yh + w) % NY
        zpair = 2 * pair(delta)
        z0 = zpair + par
        z1 = zpair + (par + 1) % 2
        for part in range(2):
            for h in range(2):
                o0 = pl.multiple_of((y * 16 + z0 * 2 + h) * 128, 128)
                o1 = pl.multiple_of((y * 16 + z1 * 2 + h) * 128, 128)
                t0 = dv[part, :, pl.ds(o0, 128)].astype(jnp.float32)
                t1 = dv[part, :, pl.ds(o1, 128)].astype(jnp.float32)
                even = jnp.where(low, t0, pltpu.roll(t1, 64, 1))
                odd = jnp.where(low, pltpu.roll(t0, 64, 1), t1)
                sbuf[p, 2 * h, part * G:(part + 1) * G, :] = even.astype(jnp.bfloat16)
                sbuf[p, 2 * h + 1, part * G:(part + 1) * G, :] = odd.astype(jnp.bfloat16)
        dbuf[p, 0] = sbuf[p, x]

    def send(src, dst, ss, rs, device):
        pltpu.make_async_remote_copy(src_ref=src, dst_ref=dst, send_sem=ss, recv_sem=rs, device_id=device,
                                     device_id_type=MESH).start()

    def wait(ref, sem):
        pltpu.make_async_copy(ref, ref, sem).wait()

    def spread(p):
        for r in range(1, NX):
            send(sbuf.at[p, (x + r) % NX], dbuf.at[p, r], ds, dr.at[p], beside(r))

    with jax.named_scope("pack0"):
        pack(0)
    with jax.named_scope("bar_wait"):
        pl.semaphore_wait(bar, len(peers) + met(1))

    for q in range(1, 4):
        ylq, cq = mates(q)
        send(wpart.at[ylq * 2 + cq], s1buf.at[q - 1], s1s, s1r, place(x, yh, z, ylq, cq))
    for p in range(EARLY):
        if p > 0:
            pack(p)
        spread(p)
    greet(ready.at[0], 1)
    with jax.named_scope("packs"):
        for p in range(EARLY, NP):
            pack(p)
    with jax.named_scope("ready0"):
        pl.semaphore_wait(ready.at[0], met(1))
    greet(ready.at[1], 2)
    with jax.named_scope("s1_wait"):
        wait(s1buf, s1r)
    total = wpart[ta].astype(jnp.float32)
    for q in range(3):
        total = total + s1buf[q].astype(jnp.float32)
    fbuf[0, yl, c] = total.astype(jnp.bfloat16)
    mine = fbuf.at[0, yl, c]
    for n in range(1, 2 * NX):
        r, u = n // 2, n % 2
        send(mine, fbuf.at[r, yl, c], fs, fr, place((x + r) % NX, yh, z, (yl + u) % 2, c))
    for p in range(EARLY, NP):
        spread(p)
    with jax.named_scope("ready1"):
        pl.semaphore_wait(ready.at[1], met(2))
    greet(ready.at[2], 4)
    with jax.named_scope("rows_wait"):
        wait(spare.at[0:2 * NX - 1], fr)
    send(fbuf.at[:, :, c], fbuf.at[:, :, c], ts, tr, twin)
    with jax.named_scope("across_wait"):
        wait(spare, tr)
    for r in range(NX):
        re = fbuf[r, 0].reshape(G, RBP)
        im = fbuf[r, 1].reshape(G, RBP)
        fstack[r * 2 * G:r * 2 * G + G, :RBP] = re
        fstack[r * 2 * G:r * 2 * G + G, RBP:] = -im
        fstack[r * 2 * G + G:(r + 1) * 2 * G, :RBP] = im
        fstack[r * 2 * G + G:(r + 1) * 2 * G, RBP:] = re


    def consume(m):
        with jax.named_scope(f"square_wait{m}"):
            wait(crecv.at[m, 1:4], cr.at[m])
        block = keep[m]
        for e in range(1, 4):
            block = block + crecv[m, e].astype(jnp.float32)
        if m == 0:
            return block
        if m == ORDER[0][0]:
            with jax.named_scope("ready2"):
                pl.semaphore_wait(ready.at[2], met(4))
        zsend[m] = block.astype(jnp.bfloat16)
        send(zsend.at[m], zrecv.at[m], zs, zr, along(m))
        return None

    for p, (m, w) in enumerate(ORDER):
        with jax.named_scope(f"piece_wait{p}"):
            wait(dbuf.at[p, 1:NX], dr.at[p])
        cols = dbuf[p].reshape(NX * 2 * G, 128)
        prod = lax.dot_general(cols, fstack[...], (((0,), (0,)), ((), ())), preferred_element_type=jnp.float32)
        for e in (2 * w + 1, 2 * w):
            block = prod[e % 2 * 64:(e % 2 + 1) * 64]
            if e == 0:
                keep[m] = block
            else:
                csend[m, e] = block.astype(jnp.bfloat16)
                send(csend.at[m, e], crecv.at[m, e], cs, cr.at[m], square(e))
        for done in SUMS.get(p, ()):
            acc = consume(done)
    with jax.named_scope("zwait"):
        wait(zrecv.at[1:4], zr)
    for m in range(1, 4):
        acc = acc + zrecv[m].astype(jnp.float32)
    out_ref[:, 0, :] = acc[:, :RB]
    out_ref[:, 1, :] = acc[:, RBP:RBP + RB]
    with jax.named_scope("send_waits"):
        wait(s1buf, s1s)
        wait(spare.at[0:2 * NX - 1], fs)
        wait(spare, ts)
        wait(dbuf.at[:, 1:NX], ds)
        wait(csend.at[:, 1:4], cs)
        wait(zsend.at[1:4], zs)


def body(density, coulomb, row_block):
    dma = pltpu.SemaphoreType.DMA
    bf16, f32 = jnp.bfloat16, jnp.float32
    out = pl.pallas_call(
        kernel,
        out_shape=pltpu.VMEM((64, 2, RB), f32),
        in_specs=[pl.BlockSpec(memory_space=pltpu.HBM)] * 3,
        out_specs=pl.BlockSpec(memory_space=pltpu.VMEM),
        scratch_shapes=[
            pltpu.SMEM((1,), jnp.int32),
            pltpu.VMEM((1, G), f32),
            pltpu.VMEM((2, G, COLS), bf16),
            pltpu.VMEM((4, Q, RBP), bf16),
            pltpu.VMEM((3, Q, RBP), bf16),
            pltpu.VMEM((NX, 2, 2, Q, RBP), bf16),
            pltpu.VMEM((2 * NX, Q, RBP), bf16),
            pltpu.VMEM((NX * 2 * G, 2 * RBP), bf16),
            pltpu.VMEM((NP, NX, 2 * G, 128), bf16),
            pltpu.VMEM((NP, NX, 2 * G, 128), bf16),
            pltpu.VMEM((4, 4, 64, 2 * RBP), bf16),
            pltpu.VMEM((4, 4, 64, 2 * RBP), bf16),
            pltpu.VMEM((4, 64, 2 * RBP), f32),
            pltpu.VMEM((4, 64, 2 * RBP), bf16),
            pltpu.VMEM((4, 64, 2 * RBP), bf16),
            dma((3,)), pltpu.SemaphoreType.REGULAR((3,)), dma, dma, dma, dma, dma, dma,
            dma, dma((NP,)), dma, dma((4,)), dma, dma,
        ],
        compiler_params=pltpu.CompilerParams(collective_id=0, has_side_effects=True),
        name="exchange",
    )(row_block, coulomb.reshape(1, G), density)
    return out.reshape(1, 64, 2, RB)


def solution(mesh):
    return jax.shard_map(
        body,
        mesh=mesh,
        in_specs=(P(None, "ga", "ta"), P("ga"), P()),
        out_specs=P("ta", "ga", None, None),
        check_vma=False,
    )
```

time: 41.1 us -> 39.4 us (0.959)
  Pallas kernels: 39.7 us -> 37.9 us
    pallas_call x1, Pallas kernels: 39.7 us -> 37.9 us  [body(): pl.pallas_call(kernel, out_shape=pltpu.VMEM((64, 2, RB), f32), in_specs=[...]
where the time goes in v5:
time: 39.4 us; the launch traced here: 39.3 us
  Pallas kernels  37.9 us (96%)
  local copies, waits for them, and re-layouts  0.66 us (2%)
  between operations  0.66 us (2%)
    pallas_call x1, Pallas kernels, body(): pl.pallas_call(kernel, out_shape=pltpu.VMEM((64, 2, RB), f32), in_specs=[...  37.9 us

profile of v5, /device:TPU:16, one launch (start us, length us, event | category | flops | bytes accessed | tf_op | source)
XLA Modules:
  0.0 39.3 jit_solution(10534241438277239639)
XLA Ops:
  0.7 37.9 %exchange.1 = f32[64,2,240]{2,1,0:T(2,128)S(1)} custom-call(s32[1]{0:T(128)S(6)} %copy.6.row_hbm, f32[1,96]{1,0:T(1,128)} %bitcast.3, bf16[2,96,4096]{2,1,0:T(8,128)(2,1)} %dens_ref.1), custom_call_target="tpu_custom_call" | custom-call | tf_op jit(solution)/shard_map/exchange/pallas_call | solution.py:224
  38.6 0.7 %copy.5 = f32[1,64,2,240]{3,2,1,0:T(2,128)} copy(f32[1,64,2,240]{3,2,1,0:T(2,128)S(1)} %bitcast.2) | data formatting | bytes 245760

commit v6 on v5

--- a/solution.py
+++ b/solution.py
@@ -13,7 +13,7 @@
 WIN = 384
 NX, NY, NZ = 4, 2, 8
 Q = 48
-ORDER = ((2, 1), (2, 0), (3, 1), (1, 1), (3, 0), (1, 0), (0, 1), (0, 0))
+ORDER = ((2, 1), (2, 0), (1, 1), (3, 1), (3, 0), (1, 0), (0, 1), (0, 0))
 NP = len(ORDER)
 SUMS = {4: (2,), 5: (3,), 6: (1,), 7: (0,)}
 EARLY = 1

time: 39.4 us -> 38.3 us (0.972)
  Pallas kernels: 37.9 us -> 36.8 us
    pallas_call x1, Pallas kernels: 37.9 us -> 36.8 us  [body(): pl.pallas_call(kernel, out_shape=pltpu.VMEM((64, 2, RB), f32), in_specs=[...]
where the time goes in v6:
time: 38.3 us; the launch traced here: 38.1 us
  Pallas kernels  36.8 us (96%)
  local copies, waits for them, and re-layouts  0.66 us (2%)
  between operations  0.66 us (2%)
    pallas_call x1, Pallas kernels, body(): pl.pallas_call(kernel, out_shape=pltpu.VMEM((64, 2, RB), f32), in_specs=[...  36.8 us

profile of v6, /device:TPU:16, one launch (start us, length us, event | category | flops | bytes accessed | tf_op | source)
XLA Modules:
  0.0 38.1 jit_solution(7377739021261512039)
XLA Ops:
  0.7 36.8 %exchange.1 = f32[64,2,240]{2,1,0:T(2,128)S(1)} custom-call(s32[1]{0:T(128)S(6)} %copy.6.row_hbm, f32[1,96]{1,0:T(1,128)} %bitcast.3, bf16[2,96,4096]{2,1,0:T(8,128)(2,1)} %dens_ref.1), custom_call_target="tpu_custom_call" | custom-call | tf_op jit(solution)/shard_map/exchange/pallas_call | solution.py:224
  37.4 0.7 %copy.5 = f32[1,64,2,240]{3,2,1,0:T(2,128)} copy(f32[1,64,2,240]{3,2,1,0:T(2,128)S(1)} %bitcast.2) | data formatting | bytes 245760

commit v7 on v6

--- a/solution.py
+++ b/solution.py
@@ -12,11 +12,12 @@
 COLS = 4096
 WIN = 384
 NX, NY, NZ = 4, 2, 8
-Q = 48
-ORDER = ((2, 1), (2, 0), (1, 1), (3, 1), (3, 0), (1, 0), (0, 1), (0, 0))
+FAR = (2, 1, 3)
+STEPS = ("O2", "W2", "O1", "O3", "W3", "C2", "W1", "C3", "O0", "C1", "W0", "C0")
+VIA = {2: 1, 3: 3, 1: 1}
+ORDER = tuple((int(step[1]), int(step[0] == "O")) for step in STEPS if step[0] in "OW")
 NP = len(ORDER)
-SUMS = {4: (2,), 5: (3,), 6: (1,), 7: (0,)}
-EARLY = 1
+EARLY = 2
 
 
 def place(x, yh, z, yl, c):
@@ -56,7 +57,7 @@
 
     bar = pltpu.get_barrier_semaphore()
     peers = [square(2), square(3)] + [place(x, yh, z, *mates(q)) for q in range(1, 4)]
-    peers += [place((x + r) % NX, yh, z, (yl + u) % 2, c) for r in range(1, NX) for u in range(2)]
+    peers += [beside(r) for r in range(1, NX)]
     for peer in peers:
         pl.semaphore_signal(bar, inc=1, device_id=peer, device_id_type=MESH)
 
@@ -91,9 +92,7 @@
         for k in range(1, (COLS - WIN) // 128 + 1):
             window = jnp.where(tile == k, dv[part, :, k * 128:k * 128 + WIN], window)
         picked = jnp.dot(window, onehot, preferred_element_type=jnp.float32)
-        weighted = (weight * picked).astype(jnp.bfloat16)
-        wpart[2 * part] = weighted[:Q]
-        wpart[2 * part + 1] = weighted[Q:]
+        wpart[part] = (weight * picked).astype(jnp.bfloat16)
 
     low = lax.broadcasted_iota(jnp.int32, (G, 128), 1) < 64
 
@@ -133,7 +132,7 @@
 
     for q in range(1, 4):
         ylq, cq = mates(q)
-        send(wpart.at[ylq * 2 + cq], s1buf.at[q - 1], s1s, s1r, place(x, yh, z, ylq, cq))
+        send(wpart.at[cq], s1buf.at[q - 1], s1s, s1r, place(x, yh, z, ylq, cq))
     for p in range(EARLY):
         if p > 0:
             pack(p)
@@ -147,71 +146,99 @@
     greet(ready.at[1], 2)
     with jax.named_scope("s1_wait"):
         wait(s1buf, s1r)
-    total = wpart[ta].astype(jnp.float32)
+    total = wpart[c].astype(jnp.float32)
     for q in range(3):
         total = total + s1buf[q].astype(jnp.float32)
-    fbuf[0, yl, c] = total.astype(jnp.bfloat16)
-    mine = fbuf.at[0, yl, c]
-    for n in range(1, 2 * NX):
-        r, u = n // 2, n % 2
-        send(mine, fbuf.at[r, yl, c], fs, fr, place((x + r) % NX, yh, z, (yl + u) % 2, c))
+    fbuf[0, c] = total.astype(jnp.bfloat16)
+    for r in FAR:
+        send(fbuf.at[0, c], fbuf.at[r, c], fs, fr, beside(r))
+    wait(spare.at[1:NX], fs)
     for p in range(EARLY, NP):
         spread(p)
     with jax.named_scope("ready1"):
         pl.semaphore_wait(ready.at[1], met(2))
     greet(ready.at[2], 4)
     with jax.named_scope("rows_wait"):
-        wait(spare.at[0:2 * NX - 1], fr)
-    send(fbuf.at[:, :, c], fbuf.at[:, :, c], ts, tr, twin)
+        wait(spare.at[1:NX], fr)
+    send(fbuf.at[:, c], fbuf.at[:, c], ts, tr, twin)
     with jax.named_scope("across_wait"):
         wait(spare, tr)
     for r in range(NX):
-        re = fbuf[r, 0].reshape(G, RBP)
-        im = fbuf[r, 1].reshape(G, RBP)
-        fstack[r * 2 * G:r * 2 * G + G, :RBP] = re
-        fstack[r * 2 * G:r * 2 * G + G, RBP:] = -im
-        fstack[r * 2 * G + G:(r + 1) * 2 * G, :RBP] = im
-        fstack[r * 2 * G + G:(r + 1) * 2 * G, RBP:] = re
-
-
-    def consume(m):
-        with jax.named_scope(f"square_wait{m}"):
-            wait(crecv.at[m, 1:4], cr.at[m])
-        block = keep[m]
-        for e in range(1, 4):
-            block = block + crecv[m, e].astype(jnp.float32)
-        if m == 0:
-            return block
-        if m == ORDER[0][0]:
-            with jax.named_scope("ready2"):
-                pl.semaphore_wait(ready.at[2], met(4))
-        zsend[m] = block.astype(jnp.bfloat16)
-        send(zsend.at[m], zrecv.at[m], zs, zr, along(m))
-        return None
-
-    for p, (m, w) in enumerate(ORDER):
+        re = fbuf[r, 0].astype(jnp.float32)[:, :RB]
+        im = fbuf[r, 1].astype(jnp.float32)[:, :RB]
+        none = jnp.zeros((G, 2 * (RBP - RB)), jnp.float32)
+        fstack[r * 2 * G:r * 2 * G + G] = jnp.concatenate([re, -im, none], axis=1).astype(jnp.bfloat16)
+        fstack[r * 2 * G + G:(r + 1) * 2 * G] = jnp.concatenate([im, re, none], axis=1).astype(jnp.bfloat16)
+
+    lane = lax.broadcasted_iota(jnp.int32, (16, 128), 1)
+
+    def packed(block):
+        tail = block[:, 384:]
+        rest = [jnp.where(lane < 96, tail[16 * j:16 * j + 16], pltpu.roll(tail[48:], 96 - 32 * j, 1)) for j in range(3)]
+        return jnp.concatenate([block[:, :128], block[:, 128:256], block[:, 256:384], *rest], axis=0)
+
+    def unpacked(block):
+        rest = [block[192 + 16 * j:208 + 16 * j] for j in range(3)]
+        back = [pltpu.roll(rest[j], 32 * j + 32, 1) for j in range(3)]
+        last = jnp.where(lane < 32, back[0], jnp.where(lane < 64, back[1], back[2]))
+        tail = jnp.concatenate([*rest, last], axis=0)
+        return jnp.concatenate([block[:64], block[64:128], block[128:192], tail], axis=1)
+
+    def produce(p):
+        m, w = ORDER[p]
         with jax.named_scope(f"piece_wait{p}"):
             wait(dbuf.at[p, 1:NX], dr.at[p])
         cols = dbuf[p].reshape(NX * 2 * G, 128)
         prod = lax.dot_general(cols, fstack[...], (((0,), (0,)), ((), ())), preferred_element_type=jnp.float32)
         for e in (2 * w + 1, 2 * w):
-            block = prod[e % 2 * 64:(e % 2 + 1) * 64]
+            block = packed(prod[e % 2 * 64:(e % 2 + 1) * 64])
             if e == 0:
                 keep[m] = block
             else:
                 csend[m, e] = block.astype(jnp.bfloat16)
-                send(csend.at[m, e], crecv.at[m, e], cs, cr.at[m], square(e))
-        for done in SUMS.get(p, ()):
-            acc = consume(done)
-    with jax.named_scope("zwait"):
-        wait(zrecv.at[1:4], zr)
-    for m in range(1, 4):
+                send(csend.at[m, e], crecv.at[m, e], cs, cr.at[m, e], square(e))
+
+    def consume(m):
+        block = keep[m]
+        for e in (2, 1, 3):
+            with jax.named_scope(f"square_wait{m}"):
+                wait(crecv.at[m, e], cr.at[m, e])
+            block = block + crecv[m, e].astype(jnp.float32)
+        if m == 0:
+            return block
+        if m == 3:
+            with jax.named_scope("via_wait"):
+                wait(zrecv.at[2], zr.at[2])
+            block = block + zrecv[2].astype(jnp.float32)
+        zsend[m] = block.astype(jnp.bfloat16)
+        send(zsend.at[m], zrecv.at[m], zs, zr.at[m], along(VIA[m]))
+        return None
+
+    piece = 0
+    greeted = False
+    for step in STEPS:
+        m = int(step[1])
+        if step[0] == "C":
+            if not greeted:
+                greeted = True
+                with jax.named_scope("ready2"):
+                    pl.semaphore_wait(ready.at[2], met(4))
+            if m == 0:
+                acc = consume(m)
+            else:
+                consume(m)
+        else:
+            produce(piece)
+            piece += 1
+    for m in (3, 1):
+        with jax.named_scope(f"zwait{m}"):
+            wait(zrecv.at[m], zr.at[m])
         acc = acc + zrecv[m].astype(jnp.float32)
-    out_ref[:, 0, :] = acc[:, :RB]
-    out_ref[:, 1, :] = acc[:, RBP:RBP + RB]
+    full = unpacked(acc)
+    out_ref[:, 0, :] = full[:, :RB]
+    out_ref[:, 1, :] = pltpu.roll(full, 2 * RBP - RB, 1)[:, :RB]
     with jax.named_scope("send_waits"):
         wait(s1buf, s1s)
-        wait(spare.at[0:2 * NX - 1], fs)
         wait(spare, ts)
         wait(dbuf.at[:, 1:NX], ds)
         wait(csend.at[:, 1:4], cs)
@@ -230,20 +257,20 @@
             pltpu.SMEM((1,), jnp.int32),
             pltpu.VMEM((1, G), f32),
             pltpu.VMEM((2, G, COLS), bf16),
-            pltpu.VMEM((4, Q, RBP), bf16),
-            pltpu.VMEM((3, Q, RBP), bf16),
-            pltpu.VMEM((NX, 2, 2, Q, RBP), bf16),
-            pltpu.VMEM((2 * NX, Q, RBP), bf16),
+            pltpu.VMEM((2, G, RBP), bf16),
+            pltpu.VMEM((3, G, RBP), bf16),
+            pltpu.VMEM((NX, 2, G, RBP), bf16),
+            pltpu.VMEM((NX, G, RBP), bf16),
             pltpu.VMEM((NX * 2 * G, 2 * RBP), bf16),
             pltpu.VMEM((NP, NX, 2 * G, 128), bf16),
             pltpu.VMEM((NP, NX, 2 * G, 128), bf16),
-            pltpu.VMEM((4, 4, 64, 2 * RBP), bf16),
-            pltpu.VMEM((4, 4, 64, 2 * RBP), bf16),
-            pltpu.VMEM((4, 64, 2 * RBP), f32),
-            pltpu.VMEM((4, 64, 2 * RBP), bf16),
-            pltpu.VMEM((4, 64, 2 * RBP), bf16),
+            pltpu.VMEM((4, 4, 240, 128), bf16),
+            pltpu.VMEM((4, 4, 240, 128), bf16),
+            pltpu.VMEM((4, 240, 128), f32),
+            pltpu.VMEM((4, 240, 128), bf16),
+            pltpu.VMEM((4, 240, 128), bf16),
             dma((3,)), pltpu.SemaphoreType.REGULAR((3,)), dma, dma, dma, dma, dma, dma,
-            dma, dma((NP,)), dma, dma((4,)), dma, dma,
+            dma, dma((NP,)), dma, dma((4, 4)), dma, dma((4,)),
         ],
         compiler_params=pltpu.CompilerParams(collective_id=0, has_side_effects=True),
         name="exchange",

time: 38.3 us -> 37.3 us (0.974)
  Pallas kernels: 36.8 us -> 35.5 us
    pallas_call x1, Pallas kernels: 36.8 us -> 35.5 us  [body(): pl.pallas_call(kernel, out_shape=pltpu.VMEM((64, 2, RB), f32), in_specs=[...]
where the time goes in v7:
time: 37.3 us; the launch traced here: 36.8 us
  Pallas kernels  35.5 us (95%)
  local copies, waits for them, and re-layouts  0.66 us (2%)
  between operations  0.66 us (2%)
    pallas_call x1, Pallas kernels, body(): pl.pallas_call(kernel, out_shape=pltpu.VMEM((64, 2, RB), f32), in_specs=[...  35.5 us

profile of v7, /device:TPU:16, one launch (start us, length us, event | category | flops | bytes accessed | tf_op | source)
XLA Modules:
  0.0 36.8 jit_solution(17236074230062191132)
XLA Ops:
  0.7 35.5 %exchange.1 = f32[64,2,240]{2,1,0:T(2,128)S(1)} custom-call(s32[1]{0:T(128)S(6)} %copy.6.row_hbm, f32[1,96]{1,0:T(1,128)} %bitcast.3, bf16[2,96,4096]{2,1,0:T(8,128)(2,1)} %dens_ref.1), custom_call_target="tpu_custom_call" | custom-call | tf_op jit(solution)/shard_map/exchange/pallas_call | solution.py:251
  36.2 0.7 %copy.5 = f32[1,64,2,240]{3,2,1,0:T(2,128)} copy(f32[1,64,2,240]{3,2,1,0:T(2,128)S(1)} %bitcast.2) | data formatting | bytes 245760

commit v8 on v7

--- a/solution.py
+++ b/solution.py
@@ -13,7 +13,7 @@
 WIN = 384
 NX, NY, NZ = 4, 2, 8
 FAR = (2, 1, 3)
-STEPS = ("O2", "W2", "O1", "O3", "W3", "C2", "W1", "C3", "O0", "C1", "W0", "C0")
+STEPS = ("O2", "W2", "O3", "O1", "W3", "C2", "W1", "C3", "O0", "C1", "W0", "C0")
 VIA = {2: 1, 3: 3, 1: 1}
 ORDER = tuple((int(step[1]), int(step[0] == "O")) for step in STEPS if step[0] in "OW")
 NP = len(ORDER)

time: 37.3 us -> 36.8 us (0.987)
  the two profiles are of different devices: /device:TPU:16 before, /device:TPU:24 now
where the time goes in v8:
time: 36.8 us; the launch traced here: 36.7 us
  Pallas kernels  35.4 us (96%)
  local copies, waits for them, and re-layouts  0.66 us (2%)
  between operations  0.66 us (2%)
    pallas_call x1, Pallas kernels, body(): pl.pallas_call(kernel, out_shape=pltpu.VMEM((64, 2, RB), f32), in_specs=[...  35.4 us

profile of v8, /device:TPU:24, one launch (start us, length us, event | category | flops | bytes accessed | tf_op | source)
XLA Modules:
  0.0 36.7 jit_solution(4014249871653609313)
XLA Ops:
  0.7 35.4 %exchange.1 = f32[64,2,240]{2,1,0:T(2,128)S(1)} custom-call(s32[1]{0:T(128)S(6)} %copy.6.row_hbm, f32[1,96]{1,0:T(1,128)} %bitcast.3, bf16[2,96,4096]{2,1,0:T(8,128)(2,1)} %dens_ref.1), custom_call_target="tpu_custom_call" | custom-call | tf_op jit(solution)/shard_map/exchange/pallas_call | solution.py:251
  36.0 0.7 %copy.5 = f32[1,64,2,240]{3,2,1,0:T(2,128)} copy(f32[1,64,2,240]{3,2,1,0:T(2,128)S(1)} %bitcast.2) | data formatting | bytes 245760

commit v9 on v8

--- a/solution.py
+++ b/solution.py
@@ -56,7 +56,7 @@
     twin = place(x, yh, z, yl, (c + 1) % 2)
 
     bar = pltpu.get_barrier_semaphore()
-    peers = [square(2), square(3)] + [place(x, yh, z, *mates(q)) for q in range(1, 4)]
+    peers = [square(2)] + [place(x, yh, z, *mates(q)) for q in range(1, 4)]
     peers += [beside(r) for r in range(1, NX)]
     for peer in peers:
         pl.semaphore_signal(bar, inc=1, device_id=peer, device_id_type=MESH)
@@ -130,7 +130,7 @@
     with jax.named_scope("bar_wait"):
         pl.semaphore_wait(bar, len(peers) + met(1))
 
-    for q in range(1, 4):
+    for q in (2, 3, 1):
         ylq, cq = mates(q)
         send(wpart.at[cq], s1buf.at[q - 1], s1s, s1r, place(x, yh, z, ylq, cq))
     for p in range(EARLY):

time: 36.8 us -> 36.4 us (0.989)
  the two profiles are of different devices: /device:TPU:24 before, /device:TPU:16 now
where the time goes in v9:
time: 36.4 us; the launch traced here: 36.3 us
  Pallas kernels  35 us (96%)
  local copies, waits for them, and re-layouts  0.66 us (2%)
  between operations  0.66 us (2%)
    pallas_call x1, Pallas kernels, body(): pl.pallas_call(kernel, out_shape=pltpu.VMEM((64, 2, RB), f32), in_specs=[...  35 us

profile of v9, /device:TPU:16, one launch (start us, length us, event | category | flops | bytes accessed | tf_op | source)
XLA Modules:
  0.0 36.3 jit_solution(385633573272397772)
XLA Ops:
  0.7 35.0 %exchange.1 = f32[64,2,240]{2,1,0:T(2,128)S(1)} custom-call(s32[1]{0:T(128)S(6)} %copy.6.row_hbm, f32[1,96]{1,0:T(1,128)} %bitcast.3, bf16[2,96,4096]{2,1,0:T(8,128)(2,1)} %dens_ref.1), custom_call_target="tpu_custom_call" | custom-call | tf_op jit(solution)/shard_map/exchange/pallas_call | solution.py:251
  35.6 0.7 %copy.5 = f32[1,64,2,240]{3,2,1,0:T(2,128)} copy(f32[1,64,2,240]{3,2,1,0:T(2,128)S(1)} %bitcast.2) | data formatting | bytes 245760

commit v10 on v9

--- a/solution.py
+++ b/solution.py
@@ -141,9 +141,6 @@
     with jax.named_scope("packs"):
         for p in range(EARLY, NP):
             pack(p)
-    with jax.named_scope("ready0"):
-        pl.semaphore_wait(ready.at[0], met(1))
-    greet(ready.at[1], 2)
     with jax.named_scope("s1_wait"):
         wait(s1buf, s1r)
     total = wpart[c].astype(jnp.float32)
@@ -152,6 +149,9 @@
     fbuf[0, c] = total.astype(jnp.bfloat16)
     for r in FAR:
         send(fbuf.at[0, c], fbuf.at[r, c], fs, fr, beside(r))
+    with jax.named_scope("ready0"):
+        pl.semaphore_wait(ready.at[0], met(1))
+    greet(ready.at[1], 2)
     wait(spare.at[1:NX], fs)
     for p in range(EARLY, NP):
         spread(p)

time: 36.4 us -> 36.4 us (level)
  no operation moved by 1% of the time
where the time goes in v10:
time: 36.4 us; the launch traced here: 36.3 us
  Pallas kernels  35 us (96%)
  local copies, waits for them, and re-layouts  0.66 us (2%)
  between operations  0.66 us (2%)
    pallas_call x1, Pallas kernels, body(): pl.pallas_call(kernel, out_shape=pltpu.VMEM((64, 2, RB), f32), in_specs=[...  35 us

profile of v10, /device:TPU:16, one launch (start us, length us, event | category | flops | bytes accessed | tf_op | source)
XLA Modules:
  0.0 36.3 jit_solution(423318125215885193)
XLA Ops:
  0.7 35.0 %exchange.1 = f32[64,2,240]{2,1,0:T(2,128)S(1)} custom-call(s32[1]{0:T(128)S(6)} %copy.6.row_hbm, f32[1,96]{1,0:T(1,128)} %bitcast.3, bf16[2,96,4096]{2,1,0:T(8,128)(2,1)} %dens_ref.1), custom_call_target="tpu_custom_call" | custom-call | tf_op jit(solution)/shard_map/exchange/pallas_call | solution.py:251
  35.6 0.7 %copy.5 = f32[1,64,2,240]{3,2,1,0:T(2,128)} copy(f32[1,64,2,240]{3,2,1,0:T(2,128)S(1)} %bitcast.2) | data formatting | bytes 245760
